TPU v7x, 32 devices: a whole 2x2x4 slice. The times are simulated.
32 devices in a mesh: grp: 4 (over y, x), dev: 8 (over z, core).
Axes of the slice: x: 2, y: 2, z: 4, core: 2. Of those that a mesh axis runs over, the one named last changes fastest.
Arguments:
- leaf_emit: float32 [3, 4096], P(None, 'dev'), may hold values from 0 to 1
- leaf_albedo: float32 [3, 4096], P(None, 'dev'), may hold values from 0.2 to 0.9
- leaf_radiosity: float32 [3, 4096], P(None, 'dev'), may hold values from 0.05 to 4
- leaf_area: float32 [4096], P('dev'), may hold values from 0.002 to 0.03
- parent_index: int32 [4096], P('dev'), may hold values from 0 to 255, as said below
- node_position: float32 [3, 6144], P(None, 'dev'), may hold values from -1 to 1
- node_angles: float32 [2, 6144], P(None, 'dev'), may hold values from -3.140625 to 3.140625
- block_receiver: int32 [4, 1024], P('grp', 'dev'), may hold values from 0 to 5
- block_source: int32 [4, 1024], P('grp', 'dev'), may hold values from 0 to 15
- block_count: int32 [4, 8], P('grp', 'dev'), may hold values from 16 to 128, as said below
Outputs:
- new_radiosity: float32 [3, 4096], P(None, 'dev')
Inputs may be any that keep to these rules, and one draw needn't show every extreme that they name: `parent_index`: within each shard's 512 leaves every cluster 0 to 255 is named at least once. The first block_count slots of a device are live, the rest are ignored. For every index of dev exactly one index of grp has 128 live slots; the others have at most 64.
All inputs are finite; a program needn't handle non-finite values.
Results may differ from a plain program's by a relative error of at most 0.0001.
Values sent between devices are 32-bit elements; how exact they have to be, the bound alone decides.
A program may use at most 64 MiB of HBM per device.

v0:
```python
import jax
import jax.numpy as jnp
from jax import lax
from jax.sharding import PartitionSpec as P

TILE = 128


batch_slots = 16


def unit_normals(node_angles):
    azimuth = node_angles[0]
    elevation = node_angles[1]
    return jnp.stack(
        [
            jnp.cos(azimuth) * jnp.cos(elevation),
            jnp.sin(azimuth) * jnp.cos(elevation),
            jnp.sin(elevation),
        ]
    )


def tile_irradiance(receivers, sources):
    offsets = [
        sources[axis_id][:, None, :] - receivers[axis_id][:, :, None] for axis_id in range(3)
    ]
    distance_sq = offsets[0] * offsets[0] + offsets[1] * offsets[1] + offsets[2] * offsets[2]
    facing_receiver = (
        receivers[3][:, :, None] * offsets[0]
        + receivers[4][:, :, None] * offsets[1]
        + receivers[5][:, :, None] * offsets[2]
    )
    facing_source = (
        sources[3][:, None, :] * offsets[0]
        + sources[4][:, None, :] * offsets[1]
        + sources[5][:, None, :] * offsets[2]
    )
    source_area = sources[6][:, None, :]
    factor = (
        source_area
        * jnp.maximum(facing_receiver, 0.0)
        * jnp.maximum(-facing_source, 0.0)
        / ((distance_sq + source_area) * (jnp.pi * distance_sq + source_area))
    )
    return jnp.einsum("bij,cbj->bci", factor, sources[7:10], precision=lax.Precision.HIGHEST)


def body(
    leaf_emit,
    leaf_albedo,
    leaf_radiosity,
    leaf_area,
    parent_index,
    node_position,
    node_angles,
    block_receiver,
    block_source,
    block_count,
):
    leaf_count = leaf_area.shape[0]
    node_count = node_position.shape[1]
    cluster_count = node_count - leaf_count
    tile_count = node_count // TILE
    slot_count = block_receiver.shape[1]
    normals = unit_normals(node_angles)
    parent_onehot = (
        parent_index[:, None] == jnp.arange(cluster_count, dtype=jnp.int32)[None, :]
    ).astype(jnp.float32)
    cluster_area = jnp.dot(leaf_area, parent_onehot, precision=lax.Precision.HIGHEST)
    weighted = jnp.dot(
        leaf_radiosity * leaf_area[None, :], parent_onehot, precision=lax.Precision.HIGHEST
    )
    cluster_radiosity = weighted / cluster_area[None, :]
    source_pack = jnp.concatenate(
        [
            node_position[:, leaf_count:],
            normals[:, leaf_count:],
            cluster_area[None, :],
            cluster_radiosity,
        ],
        axis=0,
    )
    receiver_pack = jnp.concatenate([node_position, normals], axis=0)
    linked = lax.all_to_all(receiver_pack, "dev", split_axis=1, concat_axis=1, tiled=True)
    receiver_tiles = linked.reshape(6, tile_count, TILE)
    everything = lax.all_gather(source_pack, "dev", axis=1, tiled=True)
    source_tiles = everything.reshape(10, -1, TILE)
    receiver_ids = block_receiver[0]
    source_ids = block_source[0]
    live_count = block_count[0, 0]
    step_slots = min(batch_slots, slot_count)

    def add_batch(rounds, totals):
        first = rounds * step_slots
        batch_receivers = lax.dynamic_slice_in_dim(receiver_ids, first, step_slots, 0)
        batch_sources = lax.dynamic_slice_in_dim(source_ids, first, step_slots, 0)
        batch_weight = (first + jnp.arange(step_slots, dtype=jnp.int32) < live_count).astype(
            jnp.float32
        )
        receivers = jnp.take(receiver_tiles, batch_receivers, axis=1)
        sources = jnp.take(source_tiles, batch_sources, axis=1)
        contrib = tile_irradiance(receivers, sources) * batch_weight[:, None, None]
        placement = (
            batch_receivers[:, None] == jnp.arange(tile_count, dtype=jnp.int32)[None, :]
        ).astype(jnp.float32)
        return totals + jnp.einsum(
            "bt,bci->cti", placement, contrib, precision=lax.Precision.HIGHEST
        )

    batch_total = (live_count + step_slots - 1) // step_slots
    totals = lax.fori_loop(0, batch_total, add_batch, jnp.zeros((3, tile_count, TILE), jnp.float32))
    partial_value = totals.reshape(3, node_count)
    summed = lax.psum(partial_value, "grp")
    irradiance = lax.all_to_all(summed, "dev", split_axis=1, concat_axis=1, tiled=True)
    pushed = jnp.dot(irradiance[:, leaf_count:], parent_onehot.T, precision=lax.Precision.HIGHEST)
    gathered = irradiance[:, :leaf_count] + pushed
    return leaf_emit + leaf_albedo * gathered


def solution(mesh):
    in_specs = (
        P(None, "dev"),
        P(None, "dev"),
        P(None, "dev"),
        P("dev"),
        P("dev"),
        P(None, "dev"),
        P(None, "dev"),
        P("grp", "dev"),
        P("grp", "dev"),
        P("grp", "dev"),
    )
    out_specs = P(None, "dev")
    return jax.shard_map(body, mesh=mesh, in_specs=in_specs, out_specs=out_specs, check_vma=False)
```

profile of v0, /device:TPU:0, one launch (start us, length us, event | category | flops | bytes accessed | tf_op | source)
XLA Modules:
  0.0 101.7 jit_solution(1958860069309156690)
XLA Ops:
  0.0 0.0 copy-start.2
  0.0 0.8 concatenate.17
  0.8 0.0 copy-done.2
  0.8 0.2 fusion.52
  1.0 0.1 concatenate.20
  1.1 0.1 concatenate.19
  1.2 0.1 concatenate.18
  1.2 0.6 copy.24
  1.9 6.4 %all-to-all-start = ((f32[6,8,96]{2,0,1:T(8,128)}), f32[6,8,96]{2,0,1:T(8,128)S(1)}, u32[]{:S(2)}, u32[]{:S(2)}) async-start(f32[6,8,96]{2,0,1:T(8,128)} %copy.24), calls=%async_computation | async-start | bytes 65536 | tf_op jit(solution)/shard_map/all_to_all | solution.py:85
  8.9 0.0 copy-start.7
  8.9 0.0 copy-start.6
  8.9 0.7 copy-done.7
  9.6 0.0 copy-done.6
  9.6 0.0 copy-start.3
  9.6 0.3 fusion.42
  9.9 0.4 copy-done.3
  10.3 0.3 convolution_divide_fusion
  10.6 0.0 slice-start
  10.6 0.7 slice-done
  11.3 14.5 %all_gather.3 = f32[10,2048]{1,0:T(8,128)S(1)} all-gather(f32[10,256]{1,0:T(8,128)S(1)} %fusion.48), channel_id=1, replica_groups=mesh['grp'=4,'dev'=8] {'dev'}, dimensions={1}, use_global_device_ids=true | all-gather | bytes 92160 | tf_op jit(solution)/shard_map/all_gather | solution.py:87
  25.9 0.0 all-to-all-done
  26.0 0.1 reshape.52
  26.1 0.0 copy-start
  26.1 0.0 copy-start.1
  26.1 0.6 copy-done
  26.7 0.0 copy-done.1
  26.7 18.5 %while.10 = (s32[]{:T(128)}, f32[3,6,128]{2,1,0:T(8,128)S(1)}, s32[]{:T(128)}, s32[128]{0:T(128)S(1)}, f32[10,16,128]{2,0,1:T(8,128)S(1)}, /*index=5*/s32[128]{0...) while((s32[]{:T(128)}, f32[3,6,128]{2,1,0:T(8,128)S(1)}, ...), condition=%wide.region_1.2_spmd, body=%wide.region_0.1_spmd.sunk | while | flops 17263236 | bytes 953843 | solution.py:112
  26.7 0.7 compare_and_fusion.5
  27.5 0.1 compare_and_fusion.4
  27.6 0.6 gather_fusion.1
  28.1 0.1 select_bitcast_fusion.5
  28.3 0.6 gather_fusion
  28.8 0.1 select_bitcast_fusion.4
  29.0 3.8 %convolution_multiply_fusion.2 = f32[16,3,128]{2,1,0:T(4,128)S(1)} fusion(f32[16,128]{1,0:T(8,128)S(1)} %bitcast.71, f32[16,128]{1,0:T(8,128)S(1)} %bitcast.72, f32[16,128]{1,0:T(8,128)S(1)} %bitcast.73, f32[16,128]{1,0:T(8,128)S(1)} %bitcast.78, f32[16,128]{1,0:T(8,128)S(1)} %bitcast.74, f32[16,128]{1,0:T(8,128)S(1)} %bitcast.79, ...), kind=kOutput, calls=%fused_computation.11.clone.1 | convolution fusion | flops 16783360 | bytes 164352 | tf_op jit(solution)/shard_map/while/body/bij,cbj->bci/dot_general | solution.py:46
  32.8 0.1 fusion.71
  32.9 0.7 compare_and_fusion.5
  33.6 0.1 compare_and_fusion.4
  33.7 0.6 gather_fusion.1
  34.3 0.1 select_bitcast_fusion.5
  34.5 0.6 gather_fusion
  35.0 0.1 select_bitcast_fusion.4
  35.2 3.8 %convolution_multiply_fusion.2 = f32[16,3,128]{2,1,0:T(4,128)S(1)} fusion(f32[16,128]{1,0:T(8,128)S(1)} %bitcast.71, f32[16,128]{1,0:T(8,128)S(1)} %bitcast.72, f32[16,128]{1,0:T(8,128)S(1)} %bitcast.73, f32[16,128]{1,0:T(8,128)S(1)} %bitcast.78, f32[16,128]{1,0:T(8,128)S(1)} %bitcast.74, f32[16,128]{1,0:T(8,128)S(1)} %bitcast.79, ...), kind=kOutput, calls=%fused_computation.11.clone.1 | convolution fusion | flops 16783360 | bytes 164352 | tf_op jit(solution)/shard_map/while/body/bij,cbj->bci/dot_general | solution.py:46
  38.9 0.1 fusion.71
  39.1 0.7 compare_and_fusion.5
  39.8 0.1 compare_and_fusion.4
  39.9 0.6 gather_fusion.1
  40.5 0.1 select_bitcast_fusion.5
  40.6 0.6 gather_fusion
  41.2 0.1 select_bitcast_fusion.4
  41.3 3.8 %convolution_multiply_fusion.2 = f32[16,3,128]{2,1,0:T(4,128)S(1)} fusion(f32[16,128]{1,0:T(8,128)S(1)} %bitcast.71, f32[16,128]{1,0:T(8,128)S(1)} %bitcast.72, f32[16,128]{1,0:T(8,128)S(1)} %bitcast.73, f32[16,128]{1,0:T(8,128)S(1)} %bitcast.78, f32[16,128]{1,0:T(8,128)S(1)} %bitcast.74, f32[16,128]{1,0:T(8,128)S(1)} %bitcast.79, ...), kind=kOutput, calls=%fused_computation.11.clone.1 | convolution fusion | flops 16783360 | bytes 164352 | tf_op jit(solution)/shard_map/while/body/bij,cbj->bci/dot_general | solution.py:46
  45.1 0.1 fusion.71
  45.3 0.1 all_to_all.13
  45.4 46.0 %psum.7 = f32[3,8,96]{2,1,0:T(8,128)S(1)} all-reduce(f32[3,8,96]{2,1,0:T(8,128)S(1)} %all_to_all.13), channel_id=1, replica_groups=mesh['grp'=4,'dev'=8] {'grp'}, use_global_device_ids=true, to_apply=%region_2.3 | all-reduce | flops 2304 | bytes 18432 | tf_op jit(solution)/shard_map/psum | solution.py:114
  91.3 8.7 %all_to_all.18 = f32[3,8,96]{2,0,1:T(4,128)S(1)} all-to-all(f32[3,8,96]{2,0,1:T(4,128)S(1)} %copy.28), channel_id=1, replica_groups=mesh['grp'=4,'dev'=8] {'dev'}, dimensions={1} | all-to-all | bytes 18432 | tf_op jit(solution)/shard_map/all_to_all | solution.py:115
  100.0 0.0 copy-start.4
  100.0 0.0 copy-start.5
  100.0 0.1 all_to_all.15
  100.1 0.6 copy-done.4
  100.7 0.0 copy-done.5
  100.7 1.0 fusion.41
  (25 shorter events, 0.4 us)
Async XLA Ops:
  0.0 0.8 copy-start.2
  1.9 24.1 %all-to-all-start = ((f32[6,8,96]{2,0,1:T(8,128)}), f32[6,8,96]{2,0,1:T(8,128)S(1)}, u32[]{:S(2)}, u32[]{:S(2)}) async-start(f32[6,8,96]{2,0,1:T(8,128)} %copy.24), calls=%async_computation | async-start | bytes 65536 | tf_op jit(solution)/shard_map/all_to_all | solution.py:85
  8.9 0.7 copy-start.7
  8.9 0.7 copy-start.6
  9.6 0.7 copy-start.3
  10.6 0.7 slice-start
  26.1 0.7 copy-start
  26.1 0.7 copy-start.1
  100.0 0.7 copy-start.4
  100.0 0.7 copy-start.5
where the time goes:
time: 103 us; the launch traced here: 102 us
  blocking collectives  69.2 us (67%)
  matrix products  13.3 us (13%)
  local copies, waits for them, and re-layouts  8.7 us (8%)
  starting transfers between devices  6.35 us (6%)
  other arithmetic  3.2 us (3%)
    psum x1, blocking collectives, body(): summed = lax.psum(partial_value, 'grp')  46 us
    all_gather x1, blocking collectives, body(): everything = lax.all_gather(source_pack, 'dev', axis=1, tiled=True)  14.5 us
    dot_general x3, matrix products, tile_irradiance(): jnp.einsum('bij,cbj->bci', factor, sources[7:10], precision=lax.Precision...  11.3 us
    all_to_all x1, blocking collectives, body(): lax.all_to_all(summed, 'dev', split_axis=1, concat_axis=1, tiled=True)  8.7 us
    all_to_all x1, starting transfers between devices, body(): lax.all_to_all(receiver_pack, 'dev', split_axis=1, concat_axis=1, tiled=T...  6.35 us
    unnamed x17, local copies, waits for them, and re-layouts  2.4 us
    and x3, other arithmetic, add_batch(): receivers = jnp.take(receiver_tiles, batch_receivers, axis=1)  2.19 us
  transfers between devices with their start and end apart: 1, of which 0 were waited for; matrix products, arithmetic and copies ran while one was open for 1% of the time, Pallas kernels for 0%

commit v1 on v0

--- a/solution.py
+++ b/solution.py
@@ -1,6 +1,9 @@
+import functools
 import jax
 import jax.numpy as jnp
 from jax import lax
+from jax.experimental import pallas as pl
+from jax.experimental.pallas import tpu as pltpu
 from jax.sharding import PartitionSpec as P
 
 TILE = 128
@@ -46,7 +49,7 @@
     return jnp.einsum("bij,cbj->bci", factor, sources[7:10], precision=lax.Precision.HIGHEST)
 
 
-def body(
+def listed_body(
     leaf_emit,
     leaf_albedo,
     leaf_radiosity,
@@ -118,6 +121,306 @@
     return leaf_emit + leaf_albedo * gathered
 
 
+F32 = jnp.float32
+BF16 = jnp.bfloat16
+MESH = pl.DeviceIdType.MESH
+ROWS = 10
+NT_DIMS = (((1,), (1,)), ((), ()))
+
+
+def split3(values):
+    high = values.astype(BF16)
+    rest = values - high.astype(F32)
+    middle = rest.astype(BF16)
+    low = (rest - middle.astype(F32)).astype(BF16)
+    return [high.astype(F32), middle.astype(F32), low.astype(F32)]
+
+
+def stack3(values):
+    rows = values.shape[0]
+    pad = jnp.zeros((16 - 3 * rows, values.shape[1]), F32)
+    return jnp.concatenate(split3(values) + [pad], axis=0).astype(BF16)
+
+
+def unstack3(product, rows):
+    return product[0:rows] + product[rows : 2 * rows] + product[2 * rows : 3 * rows]
+
+
+def dense_kernel(
+    groups, shards, radiosity, area, parent, position, angles, receiver_id, source_id, count,
+    out, packs, sources, columns, my_hist, hists, receivers, onehot, place, sums, part, gathered,
+    src_send, src_recv, hist_send, hist_recv, part_send, part_recv,
+):
+    g = lax.axis_index("grp")
+    k = lax.axis_index("dev")
+    device_total = groups * shards
+    me = g * shards + k
+    leaves = radiosity.shape[1]
+    nodes = position.shape[1]
+    clusters = nodes - leaves
+    per_shard = clusters // TILE
+    source_tiles = shards * per_shard
+    tiles_here = source_tiles // groups
+    per_peer = nodes // shards
+    chunks = nodes // TILE
+
+    barrier = pltpu.get_barrier_semaphore()
+
+    def greet(step, carry):
+        other = (me + step) % device_total
+        pl.semaphore_signal(
+            barrier, inc=1, device_id=(other // shards, other % shards), device_id_type=MESH
+        )
+        return carry
+
+    lax.fori_loop(1, device_total, greet, 0)
+
+    lane = lax.broadcasted_iota(jnp.int32, (1, TILE), 1)
+    code = receiver_id[...] * source_tiles + source_id[...]
+    code = jnp.where(lane < count[0, 0], code, -1)
+    square = lax.broadcasted_iota(jnp.int32, (TILE, TILE), 0)
+    hit = jnp.where(square == code, 1.0, 0.0).astype(BF16)
+    counted = lax.dot_general(
+        jnp.ones((16, TILE), BF16), hit, NT_DIMS, preferred_element_type=F32
+    )
+    my_hist[...] = counted[0:1]
+    hists[me] = counted[0:1]
+
+    ids = lax.broadcasted_iota(jnp.int32, (clusters, leaves), 0)
+    onehot[...] = jnp.where(ids == parent[...], 1.0, 0.0).astype(BF16)
+    area_row = area[...]
+    stacked = stack3(jnp.concatenate([area_row, radiosity[...] * area_row], axis=0))
+    cluster = unstack3(
+        lax.dot_general(stacked, onehot[...], NT_DIMS, preferred_element_type=F32), 4
+    )
+    cosines = jnp.cos(angles[...])
+    sines = jnp.sin(angles[...])
+    normals = [cosines[0:1] * cosines[1:2], sines[0:1] * cosines[1:2], sines[1:2]]
+    node_rows = [position[i : i + 1, :] for i in range(3)] + normals
+    for half in range(per_shard):
+        first = leaves + half * TILE
+        rows = [row[:, first : first + TILE] for row in node_rows]
+        rows.append(cluster[:, half * TILE : (half + 1) * TILE])
+        packs[half] = jnp.concatenate(rows, axis=0)
+
+    half = (g + groups * shards * per_shard - per_shard * k) % groups
+    is_owner = half < per_shard
+    mine = (per_shard * k + half) // groups
+
+    pl.semaphore_wait(barrier, device_total - 1)
+
+    def source_copy(step):
+        return pltpu.make_async_remote_copy(
+            src_ref=packs.at[half],
+            dst_ref=sources.at[mine],
+            send_sem=src_send.at[step - 1],
+            recv_sem=src_recv.at[mine],
+            device_id=(g, (k + step) % shards),
+            device_id_type=MESH,
+        )
+
+    @pl.when(is_owner)
+    def _():
+        for step in range(1, shards):
+            source_copy(step).start()
+        sources[mine] = packs[half]
+
+    def send_hist(step, carry):
+        other = (me + step) % device_total
+        pltpu.make_async_remote_copy(
+            src_ref=my_hist,
+            dst_ref=hists.at[me],
+            send_sem=hist_send,
+            recv_sem=hist_recv,
+            device_id=(other // shards, other % shards),
+            device_id_type=MESH,
+        ).start()
+        return carry
+
+    lax.fori_loop(1, device_total, send_hist, 0)
+
+    for i in range(6):
+        receivers[i] = jnp.broadcast_to(node_rows[i], (8, nodes))
+    tile_slots = TILE // source_tiles
+    node = lax.broadcasted_iota(jnp.int32, (1, nodes), 1)
+    link = jnp.zeros((1, nodes), jnp.int32)
+    for j in range(1, shards):
+        link += jnp.where(node >= j * per_peer, 1, 0)
+    spot = k * per_peer + node - link * per_peer
+    tile_of = jnp.zeros((1, nodes), jnp.int32)
+    for t in range(1, chunks):
+        tile_of += jnp.where(spot >= t * TILE, 1, 0)
+    node_key = tile_of * shards + link
+    where_rows = []
+    for t in range(tile_slots):
+        row = lax.broadcasted_iota(jnp.int32, (device_total, nodes), 0)
+        key = t * shards + row % shards
+        where_rows.append(jnp.where(key == node_key, 1.0, 0.0))
+    place[...] = jnp.concatenate(where_rows, axis=0).astype(BF16)
+
+    for m in range(tiles_here):
+        owner = (groups * m + g) // per_shard
+
+        @pl.when(k != owner)
+        def _():
+            pltpu.make_async_remote_copy(
+                src_ref=packs.at[0],
+                dst_ref=sources.at[m],
+                send_sem=src_send.at[0],
+                recv_sem=src_recv.at[m],
+                device_id=(g, owner),
+                device_id_type=MESH,
+            ).wait_recv()
+
+        padded = jnp.concatenate([sources[m], jnp.zeros((16 - ROWS, TILE), F32)], axis=0)
+        columns[...] = jnp.transpose(padded)
+
+        def add_sources(step, totals):
+            block = columns[pl.ds(pl.multiple_of(step * 8, 8), 8), :]
+            y0, y1, y2, m0, m1, m2, a, w0, w1, w2 = [
+                jnp.broadcast_to(block[:, i : i + 1], (8, TILE)) for i in range(ROWS)
+            ]
+            result = []
+            for chunk in range(chunks):
+                x0, x1, x2, n0, n1, n2 = [
+                    receivers[i, :, chunk * TILE : (chunk + 1) * TILE] for i in range(6)
+                ]
+                d0, d1, d2 = y0 - x0, y1 - x1, y2 - x2
+                r2 = d0 * d0 + d1 * d1 + d2 * d2
+                toward = jnp.maximum(n0 * d0 + n1 * d1 + n2 * d2, 0.0)
+                facing = jnp.minimum(m0 * d0 + m1 * d1 + m2 * d2, 0.0)
+                form = toward * facing / ((r2 + a) * (jnp.pi * r2 + a))
+                old = totals[3 * chunk : 3 * chunk + 3]
+                result += [old[0] - form * w0, old[1] - form * w1, old[2] - form * w2]
+            return tuple(result)
+
+        zero = jnp.zeros((8, TILE), F32)
+        totals = lax.fori_loop(0, TILE // 8, add_sources, (zero,) * (3 * chunks), unroll=2)
+        for chunk in range(chunks):
+            for c in range(3):
+                sums[3 * m + c : 3 * m + c + 1, chunk * TILE : (chunk + 1) * TILE] = jnp.sum(
+                    totals[3 * chunk + c], axis=0, keepdims=True
+                )
+
+    all_but_one = hists.at[pl.ds(0, device_total - 1)]
+    pltpu.make_async_copy(all_but_one, all_but_one, hist_recv).wait()
+    table = jnp.concatenate([hists[d] for d in range(device_total)], axis=0)
+    lanes = lax.broadcasted_iota(jnp.int32, (device_total, TILE), 1)
+    by_tile = jnp.concatenate(
+        [
+            jnp.where((lanes >= t * source_tiles) & (lanes < (t + 1) * source_tiles), table, 0.0)
+            for t in range(tile_slots)
+        ],
+        axis=0,
+    ).astype(BF16)
+    pick_row = lax.broadcasted_iota(jnp.int32, (16, TILE), 0)
+    pick_lane = lax.broadcasted_iota(jnp.int32, (16, TILE), 1)
+    pick = (pick_lane % source_tiles == groups * pick_row + g) & (pick_row < tiles_here)
+    picked = lax.dot_general(
+        jnp.where(pick, 1.0, 0.0).astype(BF16), by_tile, NT_DIMS, preferred_element_type=F32
+    )
+    weight = jnp.dot(picked.astype(BF16), place[...], preferred_element_type=F32)
+
+    irradiance = weight[0:1] * sums[0:3, :]
+    for m in range(1, tiles_here):
+        irradiance += weight[m : m + 1] * sums[3 * m : 3 * m + 3, :]
+    pushed = unstack3(
+        jnp.dot(stack3(irradiance[:, leaves:]), onehot[...], preferred_element_type=F32), 3
+    )
+    part[...] = irradiance[:, :leaves] + pushed
+    gathered[g] = irradiance[:, :leaves] + pushed
+
+    def part_copy(step):
+        return pltpu.make_async_remote_copy(
+            src_ref=part,
+            dst_ref=gathered.at[g],
+            send_sem=part_send.at[step],
+            recv_sem=part_recv.at[g],
+            device_id=((g + step) % groups, k),
+            device_id_type=MESH,
+        )
+
+    for step in range(1, groups):
+        part_copy(step).start()
+    for step in range(1, groups):
+        sender = (g + step) % groups
+        pltpu.make_async_remote_copy(
+            src_ref=part,
+            dst_ref=gathered.at[sender],
+            send_sem=part_send.at[step],
+            recv_sem=part_recv.at[sender],
+            device_id=(sender, k),
+            device_id_type=MESH,
+        ).wait_recv()
+    total = gathered[0]
+    for other in range(1, groups):
+        total += gathered[other]
+    out[...] = total
+    for step in range(1, groups):
+        part_copy(step).wait_send()
+    pltpu.make_async_copy(all_but_one, all_but_one, hist_send).wait()
+
+    @pl.when(is_owner)
+    def _():
+        for step in range(1, shards):
+            source_copy(step).wait_send()
+
+
+def dense_body(
+    groups, shards, leaf_emit, leaf_albedo, leaf_radiosity, leaf_area, parent_index,
+    node_position, node_angles, block_receiver, block_source, block_count,
+):
+    leaves = leaf_area.shape[0]
+    nodes = node_position.shape[1]
+    clusters = nodes - leaves
+    tiles_here = shards * clusters // TILE // groups
+    vmem = pl.BlockSpec(memory_space=pltpu.VMEM)
+    gathered = pl.pallas_call(
+        functools.partial(dense_kernel, groups, shards),
+        out_shape=jax.ShapeDtypeStruct((3, leaves), F32),
+        in_specs=[vmem] * 7 + [pl.BlockSpec(memory_space=pltpu.SMEM)],
+        out_specs=vmem,
+        scratch_shapes=[
+            pltpu.VMEM((clusters // TILE, ROWS, TILE), F32),
+            pltpu.VMEM((tiles_here, ROWS, TILE), F32),
+            pltpu.VMEM((TILE, 16), F32),
+            pltpu.VMEM((1, TILE), F32),
+            pltpu.VMEM((groups * shards, 1, TILE), F32),
+            pltpu.VMEM((6, 8, nodes), F32),
+            pltpu.VMEM((clusters, leaves), BF16),
+            pltpu.VMEM((TILE // (shards * clusters // TILE) * groups * shards, nodes), BF16),
+            pltpu.VMEM((3 * tiles_here, nodes), F32),
+            pltpu.VMEM((3, leaves), F32),
+            pltpu.VMEM((groups, 3, leaves), F32),
+            pltpu.SemaphoreType.DMA((shards - 1,)),
+            pltpu.SemaphoreType.DMA((tiles_here,)),
+            pltpu.SemaphoreType.DMA,
+            pltpu.SemaphoreType.DMA,
+            pltpu.SemaphoreType.DMA((groups,)),
+            pltpu.SemaphoreType.DMA((groups,)),
+        ],
+        compiler_params=pltpu.CompilerParams(collective_id=0, has_side_effects=True),
+    )(
+        leaf_radiosity, leaf_area[None, :], parent_index[None, :], node_position, node_angles,
+        block_receiver, block_source, block_count,
+    )
+    return leaf_emit + leaf_albedo * gathered
+
+
+def body(groups, shards, *args):
+    leaves, nodes, slots = args[3].shape[0], args[5].shape[1], args[7].shape[1]
+    per_shard = (nodes - leaves) // TILE
+    source_tiles = shards * per_shard
+    dense = (
+        nodes // TILE * source_tiles <= TILE
+        and TILE % source_tiles == 0
+        and source_tiles % groups == 0
+        and per_shard <= groups
+        and slots == TILE
+    )
+    return dense_body(groups, shards, *args) if dense else listed_body(*args)
+
+
 def solution(mesh):
     in_specs = (
         P(None, "dev"),
@@ -132,4 +435,5 @@
         P("grp", "dev"),
     )
     out_specs = P(None, "dev")
-    return jax.shard_map(body, mesh=mesh, in_specs=in_specs, out_specs=out_specs, check_vma=False)
+    sized = functools.partial(body, mesh.shape["grp"], mesh.shape["dev"])
+    return jax.shard_map(sized, mesh=mesh, in_specs=in_specs, out_specs=out_specs, check_vma=False)

time: 103 us -> 19.3 us (0.19); the launches traced: 102 us -> 19.1 us
  blocking collectives: 69.2 us -> 0 us
  Pallas kernels: 0 us -> 17.1 us
  matrix products: 13.3 us -> 0 us
  local copies, waits for them, and re-layouts: 8.7 us -> 0.01 us
  starting transfers between devices: 6.35 us -> 0 us
  other arithmetic: 3.2 us -> 1.3 us
    psum x1 -> x0, blocking collectives: 46 us -> none  [body(): summed = lax.psum(partial_value, 'grp')]
    pallas_call x0 -> x1, Pallas kernels: none -> 17.1 us  [dense_body(): pl.pallas_call(functools.partial(dense_kernel, groups, shards), out_shape...]
    all_gather x1 -> x0, blocking collectives: 14.5 us -> none  [body(): everything = lax.all_gather(source_pack, 'dev', axis=1, tiled=True)]
    dot_general x9 -> x0, matrix products: 13.3 us -> none  [the longest x3 11.3 us: tile_irradiance(): jnp.einsum('bij,cbj->bci', factor, sources[7:10], precision=lax.Precision...]
    all_to_all x1 -> x0, blocking collectives: 8.7 us -> none  [body(): lax.all_to_all(summed, 'dev', split_axis=1, concat_axis=1, tiled=True)]
    all_to_all x1 -> x0, starting transfers between devices: 6.35 us -> none  [body(): lax.all_to_all(receiver_pack, 'dev', split_axis=1, concat_axis=1, tiled=T...]
    gather x6 -> x0, local copies, waits for them, and re-layouts: 3.39 us -> none  [the longest x3 1.7 us: add_batch(): receivers = jnp.take(receiver_tiles, batch_receivers, axis=1)]
    and x6 -> x0, other arithmetic: 2.43 us -> none  [the longest x3 2.19 us: add_batch(): receivers = jnp.take(receiver_tiles, batch_receivers, axis=1)]
  transfers between devices with their start and end apart: 1 -> 0, of which waited for: 0 -> 0; matrix products, arithmetic and copies ran while one was open for 1% -> 0% of each run, Pallas kernels for 0% -> 0%
where the time goes in v1:
time: 19.3 us; the launch traced here: 19.1 us
  Pallas kernels  17.1 us (89%)
  other arithmetic  1.3 us (7%)
  between operations  0.69 us (4%)
    pallas_call x1, Pallas kernels, dense_body(): pl.pallas_call(functools.partial(dense_kernel, groups, shards), out_shape...  17.1 us
    add x1, other arithmetic, dense_body(): return leaf_emit + leaf_albedo * gathered  1.3 us

profile of v1, /device:TPU:0, one launch (start us, length us, event | category | flops | bytes accessed | tf_op | source)
XLA Modules:
  0.0 19.1 jit_solution(16621350993165850385)
XLA Ops:
  0.7 0.0 copy-start
  0.7 0.0 copy-start.1
  0.7 17.1 %shard_map.100 = f32[3,512]{1,0:T(4,128)} custom-call(f32[3,512]{1,0:T(4,128)} %radiosity.1, f32[1,512]{1,0:T(1,128)} %bitcast.2, s32[1,512]{1,0:T(1,128)} %bitcast.3, f32[3,768]{1,0:T(4,128)} %position.1, f32[2,768]{1,0:T(2,128)} %angles.1, s32[1,128]{1,0:T(1,128)} %receiver_id.1, s32[1,128]{1,0:T(1,128)} %source_id.1, s32[1,1]{1,0:T(1,128)S(6)} %copy.11.count), custom_call_target="tpu_custom_call" | custom-call | tf_op jit(solution)/shard_map/pallas_call | solution.py:378
  17.8 0.0 copy-done
  17.8 0.0 copy-done.1
  17.8 1.3 %multiply_add_fusion = f32[3,512]{1,0:T(4,128)} fusion(f32[3,512]{1,0:T(4,128)S(1)} %copy-done, f32[3,512]{1,0:T(4,128)S(1)} %copy-done.1, f32[3,512]{1,0:T(4,128)} %shard_map.100), kind=kLoop, calls=%fused_computation | loop fusion | flops 3072 | bytes 24576 | tf_op jit(solution)/shard_map/add | solution.py:407
Async XLA Ops:
  0.7 17.1 %copy-start = (f32[3,512]{1,0:T(4,128)S(1)}, f32[3,512]{1,0:T(4,128)}, u32[]{:S(2)}) copy-start(f32[3,512]{1,0:T(4,128)} %param.10) | copy-start | bytes 18436
  0.7 17.1 %copy-start.1 = (f32[3,512]{1,0:T(4,128)S(1)}, f32[3,512]{1,0:T(4,128)}, u32[]{:S(2)}) copy-start(f32[3,512]{1,0:T(4,128)} %param.11) | copy-start | bytes 18436

commit v2 on v1

--- a/solution.py
+++ b/solution.py
@@ -147,10 +147,14 @@
 
 
 def dense_kernel(
-    groups, shards, radiosity, area, parent, position, angles, receiver_id, source_id, count,
-    out, packs, sources, columns, my_hist, hists, receivers, onehot, place, sums, part, gathered,
-    src_send, src_recv, hist_send, hist_recv, part_send, part_recv,
+    groups, shards, *refs
 ):
+    operands, out, inputs, scratch = refs[:8], refs[8], refs[9:17], refs[17:]
+    radiosity, area, parent, position, angles, receiver_id, source_id, count = inputs
+    (
+        packs, sources, columns, my_hist, hists, receivers, onehot, place, sums, part, gathered,
+        load, src_send, src_recv, hist_send, hist_recv, part_send, part_recv,
+    ) = scratch
     g = lax.axis_index("grp")
     k = lax.axis_index("dev")
     device_total = groups * shards
@@ -166,18 +170,26 @@
 
     barrier = pltpu.get_barrier_semaphore()
 
-    def greet(step, carry):
-        other = (me + step) % device_total
-        pl.semaphore_signal(
-            barrier, inc=1, device_id=(other // shards, other % shards), device_id_type=MESH
-        )
-        return carry
-
-    lax.fori_loop(1, device_total, greet, 0)
+    far_first = sorted(range(shards), key=lambda step: -min(step, shards - step))
+    others = [
+        ((g + group_step) % groups, (k + step) % shards)
+        for step in far_first
+        for group_step in reversed(range(groups))
+        if group_step or step
+    ]
+    for other in others:
+        pl.semaphore_signal(barrier, inc=1, device_id=other, device_id_type=MESH)
+    loads = [
+        pltpu.make_async_copy(operands[i], inputs[i], load.at[i]) for i in range(len(inputs))
+    ]
+    for copy in loads:
+        copy.start()
+    for copy in loads:
+        copy.wait()
 
     lane = lax.broadcasted_iota(jnp.int32, (1, TILE), 1)
     code = receiver_id[...] * source_tiles + source_id[...]
-    code = jnp.where(lane < count[0, 0], code, -1)
+    code = jnp.where(lane < jnp.broadcast_to(count[...], (1, TILE)), code, -1)
     square = lax.broadcasted_iota(jnp.int32, (TILE, TILE), 0)
     hit = jnp.where(square == code, 1.0, 0.0).astype(BF16)
     counted = lax.dot_general(
@@ -225,19 +237,15 @@
             source_copy(step).start()
         sources[mine] = packs[half]
 
-    def send_hist(step, carry):
-        other = (me + step) % device_total
+    for other in others:
         pltpu.make_async_remote_copy(
             src_ref=my_hist,
             dst_ref=hists.at[me],
             send_sem=hist_send,
             recv_sem=hist_recv,
-            device_id=(other // shards, other % shards),
+            device_id=other,
             device_id_type=MESH,
         ).start()
-        return carry
-
-    lax.fori_loop(1, device_total, send_hist, 0)
 
     for i in range(6):
         receivers[i] = jnp.broadcast_to(node_rows[i], (8, nodes))
@@ -295,7 +303,7 @@
             return tuple(result)
 
         zero = jnp.zeros((8, TILE), F32)
-        totals = lax.fori_loop(0, TILE // 8, add_sources, (zero,) * (3 * chunks), unroll=2)
+        totals = lax.fori_loop(0, TILE // 8, add_sources, (zero,) * (3 * chunks), unroll=8)
         for chunk in range(chunks):
             for c in range(3):
                 sums[3 * m + c : 3 * m + c + 1, chunk * TILE : (chunk + 1) * TILE] = jnp.sum(
@@ -374,13 +382,17 @@
     nodes = node_position.shape[1]
     clusters = nodes - leaves
     tiles_here = shards * clusters // TILE // groups
-    vmem = pl.BlockSpec(memory_space=pltpu.VMEM)
+    operands = (
+        leaf_radiosity, leaf_area[None, :], parent_index[None, :], node_position, node_angles,
+        block_receiver, block_source, block_count,
+    )
     gathered = pl.pallas_call(
         functools.partial(dense_kernel, groups, shards),
-        out_shape=jax.ShapeDtypeStruct((3, leaves), F32),
-        in_specs=[vmem] * 7 + [pl.BlockSpec(memory_space=pltpu.SMEM)],
-        out_specs=vmem,
-        scratch_shapes=[
+        out_shape=pltpu.VMEM((3, leaves), F32),
+        in_specs=[pl.BlockSpec(memory_space=pl.ANY)] * len(operands),
+        out_specs=pl.BlockSpec(memory_space=pltpu.VMEM),
+        scratch_shapes=[pltpu.VMEM(x.shape, x.dtype) for x in operands]
+        + [
             pltpu.VMEM((clusters // TILE, ROWS, TILE), F32),
             pltpu.VMEM((tiles_here, ROWS, TILE), F32),
             pltpu.VMEM((TILE, 16), F32),
@@ -392,6 +404,7 @@
             pltpu.VMEM((3 * tiles_here, nodes), F32),
             pltpu.VMEM((3, leaves), F32),
             pltpu.VMEM((groups, 3, leaves), F32),
+            pltpu.SemaphoreType.DMA((len(operands),)),
             pltpu.SemaphoreType.DMA((shards - 1,)),
             pltpu.SemaphoreType.DMA((tiles_here,)),
             pltpu.SemaphoreType.DMA,
@@ -400,10 +413,7 @@
             pltpu.SemaphoreType.DMA((groups,)),
         ],
         compiler_params=pltpu.CompilerParams(collective_id=0, has_side_effects=True),
-    )(
-        leaf_radiosity, leaf_area[None, :], parent_index[None, :], node_position, node_angles,
-        block_receiver, block_source, block_count,
-    )
+    )(*operands)
     return leaf_emit + leaf_albedo * gathered
 
 

time: 19.3 us -> 16 us (0.83)
  Pallas kernels: 17.1 us -> 14.5 us
  other arithmetic: 1.3 us -> 0.6 us
    pallas_call x1, Pallas kernels: 17.1 us -> 14.5 us  [dense_body(): pl.pallas_call(functools.partial(dense_kernel, groups, shards), out_shape...]
    add x1, other arithmetic: 1.3 us -> 0.6 us  [dense_body(): return leaf_emit + leaf_albedo * gathered]
where the time goes in v2:
time: 16 us; the launch traced here: 15.8 us
  Pallas kernels  14.5 us (91%)
  between operations  0.69 us (4%)
  other arithmetic  0.6 us (4%)
    pallas_call x1, Pallas kernels, dense_body(): pl.pallas_call(functools.partial(dense_kernel, groups, shards), out_shape...  14.5 us
    add x1, other arithmetic, dense_body(): return leaf_emit + leaf_albedo * gathered  0.6 us

profile of v2, /device:TPU:0, one launch (start us, length us, event | category | flops | bytes accessed | tf_op | source)
XLA Modules:
  0.0 15.8 jit_solution(13665373424138567230)
XLA Ops:
  0.7 0.0 copy-start
  0.7 0.0 copy-start.1
  0.7 14.5 %shard_map.100 = f32[3,512]{1,0:T(4,128)S(1)} custom-call(f32[3,512]{1,0:T(4,128)} %refs_0_.1, f32[1,512]{1,0:T(1,128)} %bitcast.2, s32[1,512]{1,0:T(1,128)} %bitcast.3, f32[3,768]{1,0:T(4,128)} %refs_3_.1, f32[2,768]{1,0:T(2,128)} %refs_4_.1, s32[1,128]{1,0:T(1,128)} %refs_5_.1, s32[1,128]{1,0:T(1,128)} %refs_6_.1, s32[1,1]{1,0:T(1,128)S(6)} %copy.11.refs_7_), custom_call_target="tpu_custom_call" | custom-call | tf_op jit(solution)/shard_map/pallas_call | solution.py:389
  15.2 0.0 copy-done
  15.2 0.0 copy-done.1
  15.2 0.6 %multiply_add_fusion = f32[3,512]{1,0:T(4,128)} fusion(f32[3,512]{1,0:T(4,128)S(1)} %copy-done, f32[3,512]{1,0:T(4,128)S(1)} %copy-done.1, f32[3,512]{1,0:T(4,128)S(1)} %shard_map.100), kind=kLoop, calls=%fused_computation | loop fusion | flops 3072 | bytes 24576 | tf_op jit(solution)/shard_map/add | solution.py:417
Async XLA Ops:
  0.7 14.6 %copy-start = (f32[3,512]{1,0:T(4,128)S(1)}, f32[3,512]{1,0:T(4,128)}, u32[]{:S(2)}) copy-start(f32[3,512]{1,0:T(4,128)} %param.10) | copy-start | bytes 18436
  0.7 14.6 %copy-start.1 = (f32[3,512]{1,0:T(4,128)S(1)}, f32[3,512]{1,0:T(4,128)}, u32[]{:S(2)}) copy-start(f32[3,512]{1,0:T(4,128)} %param.11) | copy-start | bytes 18436

commit v3 on v2

--- a/solution.py
+++ b/solution.py
@@ -266,7 +266,9 @@
         where_rows.append(jnp.where(key == node_key, 1.0, 0.0))
     place[...] = jnp.concatenate(where_rows, axis=0).astype(BF16)
 
-    for m in range(tiles_here):
+    nearest = per_shard * k // groups
+    for turn in range(tiles_here):
+        m = (nearest + turn) % tiles_here
         owner = (groups * m + g) // per_shard
 
         @pl.when(k != owner)
@@ -306,7 +308,7 @@
         totals = lax.fori_loop(0, TILE // 8, add_sources, (zero,) * (3 * chunks), unroll=8)
         for chunk in range(chunks):
             for c in range(3):
-                sums[3 * m + c : 3 * m + c + 1, chunk * TILE : (chunk + 1) * TILE] = jnp.sum(
+                sums[3 * turn + c : 3 * turn + c + 1, chunk * TILE : (chunk + 1) * TILE] = jnp.sum(
                     totals[3 * chunk + c], axis=0, keepdims=True
                 )
 
@@ -323,7 +325,7 @@
     ).astype(BF16)
     pick_row = lax.broadcasted_iota(jnp.int32, (16, TILE), 0)
     pick_lane = lax.broadcasted_iota(jnp.int32, (16, TILE), 1)
-    pick = (pick_lane % source_tiles == groups * pick_row + g) & (pick_row < tiles_here)
+    pick = (pick_lane % source_tiles == groups * ((nearest + pick_row) % tiles_here) + g) & (pick_row < tiles_here)
     picked = lax.dot_general(
         jnp.where(pick, 1.0, 0.0).astype(BF16), by_tile, NT_DIMS, preferred_element_type=F32
     )

time: 16 us -> 16 us (level)
  no operation moved by 1% of the time
where the time goes in v3:
time: 16 us; the launch traced here: 15.8 us
  Pallas kernels  14.5 us (91%)
  between operations  0.69 us (4%)
  other arithmetic  0.6 us (4%)
    pallas_call x1, Pallas kernels, dense_body(): pl.pallas_call(functools.partial(dense_kernel, groups, shards), out_shape...  14.5 us
    add x1, other arithmetic, dense_body(): return leaf_emit + leaf_albedo * gathered  0.6 us

profile of v3, /device:TPU:0, one launch (start us, length us, event | category | flops | bytes accessed | tf_op | source)
XLA Modules:
  0.0 15.8 jit_solution(3368954160864651533)
XLA Ops:
  0.7 0.0 copy-start
  0.7 0.0 copy-start.1
  0.7 14.5 %shard_map.100 = f32[3,512]{1,0:T(4,128)S(1)} custom-call(f32[3,512]{1,0:T(4,128)} %refs_0_.1, f32[1,512]{1,0:T(1,128)} %bitcast.2, s32[1,512]{1,0:T(1,128)} %bitcast.3, f32[3,768]{1,0:T(4,128)} %refs_3_.1, f32[2,768]{1,0:T(2,128)} %refs_4_.1, s32[1,128]{1,0:T(1,128)} %refs_5_.1, s32[1,128]{1,0:T(1,128)} %refs_6_.1, s32[1,1]{1,0:T(1,128)S(6)} %copy.11.refs_7_), custom_call_target="tpu_custom_call" | custom-call | tf_op jit(solution)/shard_map/pallas_call | solution.py:391
  15.2 0.0 copy-done
  15.2 0.0 copy-done.1
  15.2 0.6 %multiply_add_fusion = f32[3,512]{1,0:T(4,128)} fusion(f32[3,512]{1,0:T(4,128)S(1)} %copy-done, f32[3,512]{1,0:T(4,128)S(1)} %copy-done.1, f32[3,512]{1,0:T(4,128)S(1)} %shard_map.100), kind=kLoop, calls=%fused_computation | loop fusion | flops 3072 | bytes 24576 | tf_op jit(solution)/shard_map/add | solution.py:419
Async XLA Ops:
  0.7 14.6 %copy-start = (f32[3,512]{1,0:T(4,128)S(1)}, f32[3,512]{1,0:T(4,128)}, u32[]{:S(2)}) copy-start(f32[3,512]{1,0:T(4,128)} %param.10) | copy-start | bytes 18436
  0.7 14.6 %copy-start.1 = (f32[3,512]{1,0:T(4,128)S(1)}, f32[3,512]{1,0:T(4,128)}, u32[]{:S(2)}) copy-start(f32[3,512]{1,0:T(4,128)} %param.11) | copy-start | bytes 18436
